TPU v7x, 32 devices: a whole 2x2x4 slice. The times are simulated.
32 devices in a mesh: fsdp: 8 (over y, x, core), tp: 4 (over z).
Axes of the slice: x: 2, y: 2, z: 4, core: 2. Of those that a mesh axis runs over, the one named last changes fastest.
Arguments:
- tokens: bfloat16 [8192, 1536], P(('fsdp', 'tp')), may hold values from -6 to 6
- cotangent: bfloat16 [8192, 1536], P(('fsdp', 'tp')), may hold values from -6 to 6
- seq_start: int32 [32], P('fsdp'), may hold values from 0 to 1, as said below
- token_valid: int32 [8192], P('fsdp'), may hold values from 0 to 1, as said below
- norm_gain: float32 [1536], replicated, may hold values from 0.5 to 1.5
- proj_z: bfloat16 [1536, 3072], P('fsdp', 'tp'), may hold values from -0.15625 to 0.15625
- proj_x: bfloat16 [1536, 3072], P('fsdp', 'tp'), may hold values from -0.15625 to 0.15625
- proj_bc: bfloat16 [1536, 256], P('fsdp'), may hold values from -0.15625 to 0.15625
- proj_dt: bfloat16 [1536, 48], P('fsdp', 'tp'), may hold values from -0.15625 to 0.15625
- conv_chan: float32 [4, 3072], P(None, 'tp'), may hold values from -3 to 3
- bias_chan: float32 [3072], P('tp'), may hold values from -0.5 to 0.5
- conv_shared: float32 [4, 256], replicated, may hold values from -3 to 3
- bias_shared: float32 [256], replicated, may hold values from -0.5 to 0.5
- a_log: float32 [48], P('tp'), may hold values from -1 to 1.5
- dt_bias: float32 [48], P('tp'), may hold values from -8 to -2
- skip_gain: float32 [48], P('tp'), may hold values from 0.5 to 1.5
- gate_gain: float32 [3072], P('tp'), may hold values from 0.5 to 1.5
- proj_out: bfloat16 [3072, 1536], P('tp', 'fsdp'), may hold values from -0.109375 to 0.109375
Outputs:
- output: bfloat16 [8192, 1536], P(('fsdp', 'tp'))
- grad_tokens: bfloat16 [8192, 1536], P(('fsdp', 'tp'))
- grad_norm_gain: float32 [1536], replicated
- grad_proj_z: float32 [1536, 3072], P('fsdp', 'tp')
- grad_proj_x: float32 [1536, 3072], P('fsdp', 'tp')
- grad_proj_bc: float32 [1536, 256], P('fsdp')
- grad_proj_dt: float32 [1536, 48], P('fsdp', 'tp')
- grad_conv_chan: float32 [4, 3072], P(None, 'tp')
- grad_bias_chan: float32 [3072], P('tp')
- grad_conv_shared: float32 [4, 256], replicated
- grad_bias_shared: float32 [256], replicated
- grad_a_log: float32 [48], P('tp')
- grad_dt_bias: float32 [48], P('tp')
- grad_skip_gain: float32 [48], P('tp')
- grad_gate_gain: float32 [3072], P('tp')
- grad_proj_out: float32 [3072, 1536], P('tp', 'fsdp')
Inputs may be any that keep to these rules, and one draw needn't show every extreme that they name: `seq_start`: each buffer of 4 blocks has 1 at its first block; a sequence spans 4 to min(15, 4) blocks and no sequence crosses a buffer; after a buffer's last sequence the flags are 0; some buffer is filled with sequences to its end. `token_valid`: within a sequence all tokens are 1 except between 0 and 127 tokens at the end of its last block; every token of the blocks after a buffer's last sequence is 0.
All inputs are finite; a program needn't handle non-finite values.
Results may differ from a plain program's by a relative error of at most 0.02.
Values may be sent and summed in bfloat16 or wider, within the bound.
A program may use at most 192 MiB of HBM per device.

v0:
```python
import jax
import jax.numpy as jnp
from jax import lax
from jax.sharding import PartitionSpec as P

HEAD = 64
STATE = 128
STRETCH = 256
INNER = 3072
EPSILON = 1e-05
PRECISE = lax.Precision.HIGHEST


def causal_conv(signal, kernel, offset_bias, openings):
    length = signal.shape[0]
    tap_count = kernel.shape[0]
    padded = jnp.concatenate(
        [jnp.zeros((tap_count - 1, signal.shape[1]), jnp.float32), signal], axis=0
    )
    within = jnp.arange(length) % STRETCH
    opening = jnp.repeat(openings, STRETCH)
    result = jnp.zeros_like(signal) + offset_bias[None, :]
    for tap_index in range(tap_count):
        reach_back = tap_count - 1 - tap_index
        allowed = 1.0 - opening * (within < reach_back).astype(jnp.float32)
        result = (
            result
            + allowed[:, None] * padded[tap_index : tap_index + length] * kernel[tap_index][None, :]
        )
    return jax.nn.silu(result)


def state_scan(inputs, step_rates, decay_a, shared_b, shared_c, openings):
    seq_len, head_count, head_size = inputs.shape
    block_count = seq_len // STRETCH
    blocks_x = inputs.reshape(block_count, STRETCH, head_count, head_size)
    blocks_dt = step_rates.reshape(block_count, STRETCH, head_count)
    blocks_b = shared_b.reshape(block_count, STRETCH, shared_b.shape[1])
    blocks_c = shared_c.reshape(block_count, STRETCH, shared_c.shape[1])
    log_decay = blocks_dt * decay_a[None, None, :]
    lower = (jnp.arange(STRETCH)[:, None] >= jnp.arange(STRETCH)[None, :]).astype(jnp.float32)
    cumulative = jnp.einsum("ts,csh->cth", lower, log_decay, precision=PRECISE)
    spread = cumulative[:, :, None, :] - cumulative[:, None, :, :]
    weights = jnp.exp(jnp.where(lower[None, :, :, None] > 0, spread, -1e30))
    intersection = jnp.einsum("ctn,csn->cts", blocks_c, blocks_b, precision=PRECISE)
    scaled_x = blocks_x * blocks_dt[..., None]
    within_block = jnp.einsum(
        "ctsh,cshp->cthp", weights * intersection[..., None], scaled_x, precision=PRECISE
    )
    to_end = jnp.exp(cumulative[:, -1:, :] - cumulative)
    block_states = jnp.einsum(
        "cshp,csn->chpn", scaled_x * to_end[..., None], blocks_b, precision=PRECISE
    )
    carry_decay = jnp.exp(cumulative[:, -1, :])

    def advance(carried, block_item):
        opening, factor, fresh_state = block_item
        entering = carried * (1.0 - opening)
        return (entering * factor[:, None, None] + fresh_state, entering)

    initial = jnp.zeros((head_count, head_size, blocks_b.shape[-1]), jnp.float32)
    _, entering = lax.scan(advance, initial, (openings, carry_decay, block_states))
    across_block = (
        jnp.einsum("ctn,chpn->cthp", blocks_c, entering, precision=PRECISE)
        * jnp.exp(cumulative)[..., None]
    )
    return (within_block + across_block).reshape(seq_len, head_count, head_size)


def gated_branch(
    pre_z,
    pre_x,
    pre_bc,
    pre_dt,
    conv_chan,
    bias_chan,
    conv_shared,
    bias_shared,
    a_log,
    dt_bias,
    skip_gain,
    validity,
    openings,
):
    length = pre_x.shape[0]
    head_count = pre_dt.shape[1]
    features = causal_conv(pre_x, conv_chan, bias_chan, openings)
    shared = causal_conv(pre_bc, conv_shared, bias_shared, openings)
    step_rates = jax.nn.softplus(pre_dt + dt_bias[None, :]) * validity[:, None]
    decay_a = -jnp.exp(a_log)
    heads_x = features.reshape(length, head_count, HEAD)
    mixed_out = state_scan(
        heads_x, step_rates, decay_a, shared[:, :STATE], shared[:, STATE:], openings
    )
    mixed_out = mixed_out + skip_gain[None, :, None] * heads_x
    return mixed_out.reshape(length, head_count * HEAD) * jax.nn.silu(pre_z) * validity[:, None]


def shards(
    tokens,
    cotangent,
    seq_start,
    token_valid,
    norm_gain,
    proj_z,
    proj_x,
    proj_bc,
    proj_dt,
    conv_chan,
    bias_chan,
    conv_shared,
    bias_shared,
    a_log,
    dt_bias,
    skip_gain,
    gate_gain,
    proj_out,
):
    validity = token_valid.astype(jnp.float32)
    openings = seq_start.astype(jnp.float32)
    whole_z, whole_x, whole_bc, whole_dt, whole_out = (
        lax.all_gather(proj_z, "fsdp", axis=0, tiled=True),
        lax.all_gather(proj_x, "fsdp", axis=0, tiled=True),
        lax.all_gather(proj_bc, "fsdp", axis=0, tiled=True),
        lax.all_gather(proj_dt, "fsdp", axis=0, tiled=True),
        lax.all_gather(proj_out, "fsdp", axis=1, tiled=True),
    )
    resid = tokens.astype(jnp.float32)
    rstd = lax.rsqrt(jnp.mean(resid * resid, axis=1, keepdims=True) + EPSILON)
    normed = (resid * rstd * norm_gain[None, :]).astype(jnp.bfloat16)
    normed_all = lax.all_gather(normed, "tp", axis=0, tiled=True)
    pre_z = jnp.dot(normed_all, whole_z, preferred_element_type=jnp.float32)
    pre_x = jnp.dot(normed_all, whole_x, preferred_element_type=jnp.float32)
    pre_bc = jnp.dot(normed_all, whole_bc, preferred_element_type=jnp.float32)
    pre_dt = jnp.dot(normed_all, whole_dt, preferred_element_type=jnp.float32)

    def mixer(
        in_z,
        in_x,
        in_bc,
        in_dt,
        taps_chan,
        offset_chan,
        taps_shared,
        offset_shared,
        log_rate,
        step_bias,
        direct_gain,
    ):
        return gated_branch(
            in_z,
            in_x,
            in_bc,
            in_dt,
            taps_chan,
            offset_chan,
            taps_shared,
            offset_shared,
            log_rate,
            step_bias,
            direct_gain,
            validity,
            openings,
        )

    gated, mixer_back = jax.vjp(
        mixer,
        pre_z,
        pre_x,
        pre_bc,
        pre_dt,
        conv_chan,
        bias_chan,
        conv_shared,
        bias_shared,
        a_log,
        dt_bias,
        skip_gain,
    )
    squares = lax.psum(jnp.sum(gated * gated, axis=1), "tp")
    gate_rstd = lax.rsqrt(squares / INNER + EPSILON)[:, None]
    gnormed = (gated * gate_rstd * gate_gain[None, :]).astype(jnp.bfloat16)
    mixed = lax.psum_scatter(
        jnp.dot(gnormed, whole_out, preferred_element_type=jnp.float32).astype(jnp.bfloat16),
        "tp",
        scatter_dimension=0,
        tiled=True,
    ).astype(jnp.float32)
    cot_all = lax.all_gather(cotangent, "tp", axis=0, tiled=True)
    d_gnormed = jnp.einsum("td,cd->tc", cot_all, whole_out, preferred_element_type=jnp.float32)
    grad_out_rows = jnp.einsum("tc,td->cd", gnormed, cot_all, preferred_element_type=jnp.float32)
    output = (resid + mixed).astype(jnp.bfloat16)
    scaled = gate_gain[None, :] * d_gnormed
    d_gate_gain = jnp.sum(d_gnormed * gated * gate_rstd, axis=0)
    cross = lax.psum(jnp.sum(scaled * gated, axis=1), "tp")
    d_gated = (
        gate_rstd * scaled - gated * (gate_rstd * gate_rstd * gate_rstd) * (cross / INNER)[:, None]
    )
    grads = mixer_back(d_gated)
    grad_z = grads[0].astype(jnp.bfloat16)
    grad_x = grads[1].astype(jnp.bfloat16)
    grad_bc = grads[2].astype(jnp.bfloat16)
    grad_dt = grads[3].astype(jnp.bfloat16)
    weight_z = jnp.einsum("td,tc->dc", normed_all, grad_z, preferred_element_type=jnp.float32)
    weight_x = jnp.einsum("td,tc->dc", normed_all, grad_x, preferred_element_type=jnp.float32)
    weight_bc = jnp.einsum("td,tc->dc", normed_all, grad_bc, preferred_element_type=jnp.float32)
    weight_dt = jnp.einsum("td,tc->dc", normed_all, grad_dt, preferred_element_type=jnp.float32)

    def partial_term(grad_rows, weight_full):
        return jnp.einsum("tc,dc->td", grad_rows, weight_full, preferred_element_type=jnp.float32)

    d_normed = lax.psum_scatter(
        (
            partial_term(grad_z, whole_z)
            + partial_term(grad_x, whole_x)
            + partial_term(grad_bc, whole_bc)
            + partial_term(grad_dt, whole_dt)
        ).astype(jnp.bfloat16),
        "tp",
        scatter_dimension=0,
        tiled=True,
    ).astype(jnp.float32)
    owned_z, owned_x, owned_bc, owned_dt, owned_out = (
        lax.psum_scatter(
            weight_z.astype(jnp.bfloat16), "fsdp", scatter_dimension=0, tiled=True
        ).astype(jnp.float32),
        lax.psum_scatter(
            weight_x.astype(jnp.bfloat16), "fsdp", scatter_dimension=0, tiled=True
        ).astype(jnp.float32),
        lax.psum_scatter(
            weight_bc.astype(jnp.bfloat16), "fsdp", scatter_dimension=0, tiled=True
        ).astype(jnp.float32),
        lax.psum_scatter(
            weight_dt.astype(jnp.bfloat16), "fsdp", scatter_dimension=0, tiled=True
        ).astype(jnp.float32),
        lax.psum_scatter(
            grad_out_rows.astype(jnp.bfloat16), "fsdp", scatter_dimension=1, tiled=True
        ).astype(jnp.float32),
    )
    d_norm_gain = jnp.sum(d_normed * resid * rstd, axis=0)
    scaled_in = d_normed * norm_gain[None, :]
    d_resid = rstd * scaled_in - resid * (rstd * rstd * rstd) * jnp.mean(
        scaled_in * resid, axis=1, keepdims=True
    )
    grad_tokens = (d_resid + cotangent.astype(jnp.float32)).astype(jnp.bfloat16)
    summed = lax.psum(
        (
            grads[4],
            grads[5],
            grads[6],
            grads[7],
            grads[8],
            grads[9],
            grads[10],
            d_gate_gain,
            d_norm_gain,
        ),
        "fsdp",
    )
    shared_sums = (
        lax.psum(owned_bc.astype(jnp.bfloat16), "tp").astype(jnp.float32),
        lax.psum(summed[2].astype(jnp.bfloat16), "tp").astype(jnp.float32),
        lax.psum(summed[3].astype(jnp.bfloat16), "tp").astype(jnp.float32),
        lax.psum(summed[8].astype(jnp.bfloat16), "tp").astype(jnp.float32),
    )
    return (
        output,
        grad_tokens,
        shared_sums[3],
        owned_z,
        owned_x,
        shared_sums[0],
        owned_dt,
        summed[0],
        summed[1],
        shared_sums[1],
        shared_sums[2],
        summed[4],
        summed[5],
        summed[6],
        summed[7],
        owned_out,
    )


def solution(mesh):
    in_specs = (
        P(("fsdp", "tp"), None),
        P(("fsdp", "tp"), None),
        P("fsdp"),
        P("fsdp"),
        P(),
        P("fsdp", "tp"),
        P("fsdp", "tp"),
        P("fsdp", None),
        P("fsdp", "tp"),
        P(None, "tp"),
        P("tp"),
        P(),
        P(),
        P("tp"),
        P("tp"),
        P("tp"),
        P("tp"),
        P("tp", "fsdp"),
    )
    out_specs = (
        P(("fsdp", "tp"), None),
        P(("fsdp", "tp"), None),
        P(),
        P("fsdp", "tp"),
        P("fsdp", "tp"),
        P("fsdp", None),
        P("fsdp", "tp"),
        P(None, "tp"),
        P("tp"),
        P(),
        P(),
        P("tp"),
        P("tp"),
        P("tp"),
        P("tp"),
        P("tp", "fsdp"),
    )
    return jax.shard_map(shards, mesh=mesh, in_specs=in_specs, out_specs=out_specs, check_vma=False)
```

profile of v0, /device:TPU:0, one launch (start us, length us, event | category | flops | bytes accessed | tf_op | source)
XLA Modules:
  0.0 749.7 jit_solution(2506165639398660441)
XLA Ops:
  16.0 10.7 %all-gather = bf16[8,192,12]{1,2,0:T(8,128)(2,1)S(1)} all-gather(bf16[1,192,12]{1,2,0:T(8,128)(2,1)S(1)} %bitcast.207), channel_id=1, replica_groups=mesh['fsdp'=8,'tp'=4] {'fsdp'}, dimensions={0}, use_global_device_ids=true | all-gather | bytes 41472 | tf_op jit(solution)/shard_map/all_gather | solution.py:125
  26.9 10.4 %all_gather.24 = bf16[1536,256]{1,0:T(8,128)(2,1)S(1)} all-gather(bf16[192,256]{1,0:T(8,128)(2,1)S(1)} %copy-done.48), channel_id=1, replica_groups=mesh['fsdp'=8,'tp'=4] {'fsdp'}, dimensions={0}, use_global_device_ids=true | all-gather | bytes 884736 | tf_op jit(solution)/shard_map/all_gather | solution.py:124
  37.2 41.2 %all-gather.7.cloned.1.call-done = bf16[1024,1536]{1,0:T(8,128)(2,1)} async-done(((bf16[256,1536]{1,0:T(8,128)(2,1)}), bf16[1024,1536]{1,0:T(8,128)(2,1)}) %all-gather.7.cloned.1.call-update) | async-done | bytes 3145744 | tf_op jit(solution)/shard_map/all_gather | solution.py:131
  87.6 20.3 %all-gather.9.cloned.1.call-done = bf16[1536,768]{1,0:T(8,128)(2,1)} async-done(((bf16[192,768]{1,0:T(8,128)(2,1)}), bf16[1536,768]{1,0:T(8,128)(2,1)}) %all-gather.9.cloned.1.call-update) | async-done | bytes 2359312 | tf_op jit(solution)/shard_map/all_gather | solution.py:123
  134.9 14.7 %while.36 = (s32[]{:T(128)}, f32[12,64,128]{2,1,0:T(8,128)S(1)}, f32[4,12,64,128]{3,2,1,0:T(8,128)S(1)}, f32[4]{0:T(128)S(1)}, f32[4,12,1,1]{1,3,2,0:T(1,128)}, ...) while((s32[]{:T(128)}, f32[12,64,128]{2,1,0:T(8,128)S(1)}, ...), condition=%wide.region_2.3_spmd.clone, body=%wide.region_1.2_spmd.clone.sunk | while | flops 589828 | bytes 1967464 | solution.py:62
  152.4 14.1 %bitcast_add_fusion.3 = f32[4,256,12,64]{1,3,2,0:T(8,128)S(1)} fusion(f32[4,256,12,64]{1,3,2,0:T(8,128)S(1)} %fusion.123, f32[4,256,256]{2,1,0:T(8,128)S(1)} %copy-done.31, f32[4,256,12]{1,2,0:T(8,128)S(1)} %convolution_bitcast_fusion.1, pred[256,256]{1,0:T(8,128)(4,1)S(1)} %convert_compare_fusion, f32[4,256,12,64]{1,0,3,2:T(4,128)S(1)} %copy-done.6, ...), kind=kOutput, calls=%fused_computation.59 | convolution fusion | flops 2427715584 | bytes 10698752 | tf_op jit(solution)/shard_map/jvp(ctsh,cshp->cthp)/dot_general | solution.py:47
  174.6 8.9 %multiply_reduce_fusion.10 = (f32[1024]{0:T(1024)}, f32[1024,768]{1,0:T(8,128)}, f32[1024,768]{1,0:T(8,128)}) fusion(f32[1024]{0:T(1024)S(1)} %convert_element_type.114, f32[1024,768]{1,0:T(8,128)} %copy.94, f32[1024,768]{1,0:T(8,128)} %get-tuple-element.356, f32[768]{0:T(1024)} %mul.780, bf16[1024,1536]{1,0:T(8,128)(2,1)S(1)} %copy-done.1, ...), kind=kOutput, calls=%fused_computation.76 | convolution fusion | flops 2426928128 | bytes 18099200 | tf_op jit(solution)/shard_map/dot_general | solution.py:132
  183.5 12.5 %psum.105 = f32[1024]{0:T(1024)S(1)} all-reduce(f32[1024]{0:T(1024)} %get-tuple-element.353), channel_id=1, replica_groups=mesh['fsdp'=8,'tp'=4] {'tp'}, use_global_device_ids=true, to_apply=%region_4.5 | all-reduce | flops 1024 | bytes 8192 | tf_op jit(solution)/shard_map/psum | solution.py:180
  196.7 37.8 %all-gather.15.cloned.1.call-done = bf16[1024,1536]{1,0:T(8,128)(2,1)} async-done(((bf16[256,1536]{1,0:T(8,128)(2,1)}), bf16[1024,1536]{1,0:T(8,128)(2,1)}) %all-gather.15.cloned.1.call-update) | async-done | bytes 3145744 | tf_op jit(solution)/shard_map/all_gather | solution.py:189
  234.5 8.7 %multiply_reduce_fusion = (f32[768]{0:T(1024)}, f32[1024]{0:T(1024)}, f32[1024,768]{1,0:T(8,128)}) fusion(f32[1024,768]{1,0:T(8,128)} %get-tuple-element.354, f32[1024]{0:T(1024)} %get-tuple-element.382, f32[768]{0:T(1024)} %param.38, bf16[1024,1536]{1,0:T(8,128)(2,1)} %all-gather.15.cloned.1.call-done, bf16[768,1536]{0,1:T(8,128)(2,1)} %all-gather.13.cloned.1.call-done), kind=kOutput, calls=%fused_computation.60 | convolution fusion | flops 2420635904 | bytes 11810816 | tf_op jit(solution)/shard_map/td,cd->tc/dot_general | solution.py:190
  243.2 10.2 %psum.106 = f32[1024]{0:T(1024)} all-reduce(f32[1024]{0:T(1024)} %get-tuple-element.284), channel_id=1, replica_groups=mesh['fsdp'=8,'tp'=4] {'tp'}, use_global_device_ids=true, to_apply=%region_7.8 | all-reduce | flops 1024 | bytes 8192 | tf_op jit(solution)/shard_map/psum | solution.py:195
  283.3 25.8 %while.37 = (s32[]{:T(128)}, f32[12,64,128]{2,1,0:T(8,128)S(1)}, f32[4,12]{1,0:T(4,128)}, f32[4,12,64,128]{3,2,1,0:T(8,128)}, f32[4,12,64,128]{3,2,1,0:T(8,128)}...) while((s32[]{:T(128)}, f32[12,64,128]{2,1,0:T(8,128)S(1)}, ...), condition=%wide.region_10.11_spmd.clone, body=%wide.region_8.10_spmd.clone.sunk | while | flops 688120 | bytes 2359756 | solution.py:62
  322.2 18.7 %fusion.14 = (f32[4,256,12]{1,2,0:T(8,128)}, f32[4,256,12]{1,2,0:T(8,128)}, f32[4,256,256]{2,1,0:T(8,128)}) fusion(f32[4,256,256]{2,1,0:T(8,128)S(1)} %copy-done.32, f32[4,256,12]{1,2,0:T(8,128)S(1)} %copy-done.35, pred[256,256]{1,0:T(8,128)(4,1)S(1)} %copy-done.54, f32[4,256,12,64]{1,0,3,2:T(4,128)S(1)} %copy-done.7, f32[4,256,12]{1,2,0:T(8,128)S(1)} %copy-done.37, ...), kind=kOutput, calls=%fused_computation.25 | convolution fusion | flops 2444730368 | bytes 8650752 | tf_op jit(solution)/shard_map/transpose(jvp(ctsh,cshp->cthp))/dot_general | solution.py:47
  347.8 14.3 %multiply_reduce_fusion.6 = (f32[4,256,12]{1,2,0:T(8,128)S(1)}, f32[4,256,12]{1,2,0:T(8,128)}, f32[4,256,12,64]{1,3,2,0:T(8,128)}) fusion(f32[4,256,12,64]{1,3,2,0:T(8,128)} %fusion.125, f32[4,256,12,64]{1,0,3,2:T(4,128)S(1)} %copy-done.8, f32[4,256,12]{1,2,0:T(8,128)S(1)} %copy-done.37, f32[4,256,256]{2,1,0:T(8,128)S(1)} %copy-done.33, ...), kind=kOutput, calls=%fused_computation.66 | convolution fusion | flops 2431623168 | bytes 13942784 | tf_op jit(solution)/shard_map/transpose(jvp(ctsh,cshp->cthp))/dot_general | solution.py:47
  375.2 27.8 %reduce-scatter.18.cloned.1.call-done = bf16[192,256]{1,0:T(8,128)(2,1)} async-done(((bf16[1536,256]{1,0:T(8,128)(2,1)}), bf16[192,256]{1,0:T(8,128)(2,1)}) %reduce-scatter.18.cloned.1.call-update) | async-done | bytes 98320 | tf_op jit(solution)/shard_map/reduce_scatter | solution.py:230
  426.4 10.0 %multiply_reduce_fusion.5 = (f32[768]{0:T(1024)S(1)}, f32[768]{0:T(1024)S(1)}, f32[768]{0:T(1024)S(1)}, f32[768]{0:T(1024)S(1)}, f32[768]{0:T(1024)S(1)}, /*index=5*/f32[1024,768]{1,0:T(8,128)S(1)}) fusion(f32[1024,768]{1,0:T(8,128)} %copy-done.14, f32[1024]{0:T(1024)S(1)} %get-tuple-element.384, f32[1024]{0:T(1024)S(1)} %get-tuple-element.383, ...), kind=kLoop, calls=%fused_computation.65 | loop fusion | flops 18870528 | bytes 15763456 | tf_op jit(solution)/shard_map/transpose(jvp())/reduce_sum | solution.py:28
  464.9 12.5 %all-reduce.26.cloned.1.call-done = bf16[192,256]{1,0:T(8,128)(2,1)} async-done(((bf16[192,256]{1,0:T(8,128)(2,1)}), bf16[192,256]{1,0:T(8,128)(2,1)}) %all-reduce.26.cloned.1.call-update) | async-done | bytes 98320 | tf_op jit(solution)/shard_map/psum | solution.py:261
  479.0 43.9 %reduce-scatter.20.cloned.1.call-done = bf16[768,192]{0,1:T(8,128)(2,1)} async-done(((bf16[768,1536]{0,1:T(8,128)(2,1)}), bf16[768,192]{0,1:T(8,128)(2,1)}) %reduce-scatter.20.cloned.1.call-update) | async-done | bytes 294928 | tf_op jit(solution)/shard_map/reduce_scatter | solution.py:236
  524.7 43.8 %reduce-scatter.14.cloned.1.call-done = bf16[192,768]{1,0:T(8,128)(2,1)} async-done(((bf16[1536,768]{1,0:T(8,128)(2,1)}), bf16[192,768]{1,0:T(8,128)(2,1)}) %reduce-scatter.14.cloned.1.call-update) | async-done | bytes 294928 | tf_op jit(solution)/shard_map/reduce_scatter | solution.py:224
  570.2 43.9 %reduce-scatter.16.cloned.1.call-done = bf16[192,768]{1,0:T(8,128)(2,1)} async-done(((bf16[1536,768]{1,0:T(8,128)(2,1)}), bf16[192,768]{1,0:T(8,128)(2,1)}) %reduce-scatter.16.cloned.1.call-update) | async-done | bytes 294928 | tf_op jit(solution)/shard_map/reduce_scatter | solution.py:227
  616.0 60.8 %reduce-scatter.12.cloned.1.call-done = bf16[256,1536]{1,0:T(8,128)(2,1)} async-done(((bf16[1024,1536]{1,0:T(8,128)(2,1)}), bf16[256,1536]{1,0:T(8,128)(2,1)}) %reduce-scatter.12.cloned.1.call-update) | async-done | bytes 786448 | tf_op jit(solution)/shard_map/reduce_scatter | solution.py:212
  678.4 25.5 %all-reduce.22 = (bf16[1536]{0:T(1024)(128)(2,1)S(1)}, f32[4,768]{1,0:T(4,128)}, f32[768]{0:T(1024)}, bf16[4,256]{1,0:T(4,128)(2,1)S(1)}, bf16[256]{0:T(256)(128...) all-reduce(f32[1536]{0:T(1024)S(1)} %get-tuple-element.296, ...), channel_id=1, replica_groups=mesh['fsdp'=8,'tp'=4] {'fsdp'}, use_global_device_ids=true, to_apply=%region_21.22 | all-reduce | flops 7460 | bytes 54048 | tf_op jit(solution)/shard_map/psum | solution.py:246
  703.8 11.9 %all-reduce.23 = (bf16[1536]{0:T(1024)(128)(2,1)S(1)}, bf16[4,256]{1,0:T(4,128)(2,1)S(1)}, bf16[256]{0:T(256)(128)(2,1)S(1)}) all-reduce(bf16[1536]{0:T(1024)(128)(2,1)S(1)} %get-tuple-element.335, bf16[4,256]{1,0:T(4,128)(2,1)S(1)} %get-tuple-element.338, ...), channel_id=1, replica_groups=mesh['fsdp'=8,'tp'=4] {'tp'}, use_global_device_ids=true, to_apply=%region_22.23 | all-reduce | flops 2816 | bytes 11264 | tf_op jit(solution)/shard_map/psum | solution.py:264
  717.5 22.3 %reduce-scatter.10.cloned.1.call-done = bf16[256,1536]{1,0:T(8,128)(2,1)} async-done(((bf16[1024,1536]{1,0:T(8,128)(2,1)}), bf16[256,1536]{1,0:T(8,128)(2,1)}) %reduce-scatter.10.cloned.1.call-update) | async-done | bytes 786448 | tf_op jit(solution)/shard_map/reduce_scatter | solution.py:183
  (379 shorter events, 223.6 us)
Async XLA Ops:
  7.3 71.2 %all-gather.7.cloned.1.call-start = ((), (), s32[]{:S(2)}) async-start(), calls=%async_computation.7 | async-start | bytes 3932160 | tf_op jit(solution)/shard_map/all_gather | solution.py:131
  12.1 95.8 %all-gather.9.cloned.1.call-start = ((), (), s32[]{:S(2)}) async-start(), calls=%async_computation.8 | async-start | bytes 2654208 | tf_op jit(solution)/shard_map/all_gather | solution.py:123
  12.9 161.7 %all-gather.11.cloned.1.call-start = ((), (), s32[]{:S(2)}) async-start(), calls=%async_computation.9 | async-start | bytes 2654208 | tf_op jit(solution)/shard_map/all_gather | solution.py:122
  13.6 183.0 %all-gather.13.cloned.1.call-start = ((), (), s32[]{:S(2)}) async-start(), calls=%async_computation.10 | async-start | bytes 2654208 | tf_op jit(solution)/shard_map/all_gather | solution.py:126
  14.2 220.3 %all-gather.15.cloned.1.call-start = ((), (), s32[]{:S(2)}) async-start(), calls=%async_computation.12 | async-start | bytes 3932160 | tf_op jit(solution)/shard_map/all_gather | solution.py:189
  14.8 388.2 %reduce-scatter.18.cloned.1.call-start = ((), (), s32[]{:S(2)}) async-start(), calls=%async_computation.16 | async-start | bytes 884736 | tf_op jit(solution)/shard_map/reduce_scatter | solution.py:230
  14.9 137.4 %copy-start.53 = (pred[256,256]{1,0:T(8,128)(4,1)}, pred[256,256]{1,0:T(8,128)(4,1)S(1)}, u32[]{:S(2)}) copy-start(pred[256,256]{1,0:T(8,128)(4,1)S(1)} %convert_compare_fusion) | copy-start | bytes 196612
  15.9 97.2 %copy-start.43 = (f32[1024]{0:T(1024)}, f32[1024]{0:T(1024)S(1)}, u32[]{:S(2)}) copy-start(f32[1024]{0:T(1024)S(1)} %get-tuple-element.386) | copy-start | bytes 12292
  15.9 97.2 %copy-start.56 = (f32[768]{0:T(1024)}, f32[768]{0:T(1024)S(1)}, u32[]{:S(2)}) copy-start(f32[768]{0:T(1024)S(1)} %get-tuple-element.299) | copy-start | bytes 9220
  15.9 97.2 %copy-start.58 = (f32[768]{0:T(1024)}, f32[768]{0:T(1024)S(1)}, u32[]{:S(2)}) copy-start(f32[768]{0:T(1024)S(1)} %get-tuple-element.300) | copy-start | bytes 9220
  369.0 94.4 %reduce-scatter.22.cloned.1.call-start = ((), (), s32[]{:S(2)}) async-start(), calls=%async_computation.19 | async-start | bytes 442368
  375.2 102.2 %all-reduce.26.cloned.1.call-start = ((), (), s32[]{:S(2)}) async-start(), calls=%async_computation.17 | async-start | bytes 196608 | tf_op jit(solution)/shard_map/psum | solution.py:261
  403.0 119.8 %reduce-scatter.20.cloned.1.call-start = ((), (), s32[]{:S(2)}) async-start(), calls=%async_computation.18 | async-start | bytes 2654208 | tf_op jit(solution)/shard_map/reduce_scatter | solution.py:236
  410.8 157.6 %reduce-scatter.14.cloned.1.call-start = ((), (), s32[]{:S(2)}) async-start(), calls=%async_computation.14 | async-start | bytes 2654208 | tf_op jit(solution)/shard_map/reduce_scatter | solution.py:224
  416.3 197.8 %reduce-scatter.16.cloned.1.call-start = ((), (), s32[]{:S(2)}) async-start(), calls=%async_computation.15 | async-start | bytes 2654208 | tf_op jit(solution)/shard_map/reduce_scatter | solution.py:227
  443.9 232.9 %reduce-scatter.12.cloned.1.call-start = ((), (), s32[]{:S(2)}) async-start(), calls=%async_computation.13 | async-start | bytes 3932160 | tf_op jit(solution)/shard_map/reduce_scatter | solution.py:212
  454.6 285.2 %reduce-scatter.10.cloned.1.call-start = ((), (), s32[]{:S(2)}) async-start(), calls=%async_computation.11 | async-start | bytes 3932160 | tf_op jit(solution)/shard_map/reduce_scatter | solution.py:183
  462.4 214.3 %copy-start.16 = (bf16[256,1536]{1,0:T(8,128)(2,1)S(1)}, bf16[256,1536]{1,0:T(8,128)(2,1)}, u32[]{:S(2)}) copy-start(bf16[256,1536]{1,0:T(8,128)(2,1)} %param.22) | copy-start | bytes 2359300
  462.4 214.3 %copy-start.49 = (f32[1536]{0:T(1024)S(1)}, f32[1536]{0:T(1024)}, u32[]{:S(2)}) copy-start(f32[1536]{0:T(1024)} %param.26) | copy-start | bytes 18436
  462.5 214.3 %copy-start.69 = (f32[256]{0:T(256)S(1)}, f32[256]{0:T(256)}, u32[]{:S(2)}) copy-start(f32[256]{0:T(256)} %copy-done.68) | copy-start | bytes 3076
  462.5 215.9 %copy-start.84 = (f32[768]{0:T(1024)S(1)}, f32[768]{0:T(1024)}, u32[]{:S(2)}) copy-start(f32[768]{0:T(1024)} %get-tuple-element.283) | copy-start | bytes 9220
  462.5 215.8 %copy-start.87 = (f32[256]{0:T(256)S(1)}, f32[256]{0:T(256)}, u32[]{:S(2)}) copy-start(f32[256]{0:T(256)} %get-tuple-element.298) | copy-start | bytes 3076
  462.5 277.3 %copy-start.21 = (bf16[256,1536]{1,0:T(8,128)(2,1)S(1)}, bf16[256,1536]{1,0:T(8,128)(2,1)}, u32[]{:S(2)}) copy-start(bf16[256,1536]{1,0:T(8,128)(2,1)} %param.23) | copy-start | bytes 2359300
  462.5 277.3 %copy-start.83 = (f32[256]{0:T(256)S(1)}, f32[256]{0:T(256)}, u32[]{:S(2)}) copy-start(f32[256]{0:T(256)} %get-tuple-element.391) | copy-start | bytes 3076
  (92 other events, 1602.3 us)
Sparse Core Ops, SparseCore 0:
  12.3 66.1 all-gather.6
  80.3 27.5 all-gather.8
  109.8 28.8 all-gather.10
  140.4 28.9 all-gather.12
  170.8 63.6 all-gather.14
  369.1 33.7 reduce-scatter.17
  406.6 33.9 reduce-scatter.21
  442.9 34.4 all-reduce.25
  480.7 42.0 reduce-scatter.19
  526.0 42.3 reduce-scatter.13
  571.8 42.3 reduce-scatter.15
  616.3 60.3 reduce-scatter.11
  679.0 60.7 reduce-scatter.9
where the time goes:
time: 761 us; the launch traced here: 750 us
  waiting for transfers between devices  357 us (47%)
  matrix products  154 us (20%)
  blocking collectives  81.3 us (11%)
  other arithmetic  78.7 us (10%)
  local copies, waits for them, and re-layouts  61.8 us (8%)
  between operations  15.6 us (2%)
    reduce_scatter x1, waiting for transfers between devices, shards(): lax.psum_scatter((partial_term(grad_z, whole_z) + partial_term(grad_x, wh...  60.8 us
    dot_general x3, matrix products, state_scan(): jnp.einsum('ctsh,cshp->cthp', weights * intersection[..., None], scaled_x...  47.1 us
    reduce_scatter x1, waiting for transfers between devices, shards(): lax.psum_scatter(weight_x.astype(jnp.bfloat16), 'fsdp', scatter_dimension...  43.9 us
    reduce_scatter x1, waiting for transfers between devices, shards(): lax.psum_scatter(grad_out_rows.astype(jnp.bfloat16), 'fsdp', scatter_dime...  43.9 us
    reduce_scatter x1, waiting for transfers between devices, shards(): lax.psum_scatter(weight_z.astype(jnp.bfloat16), 'fsdp', scatter_dimension...  43.8 us
    all_gather x1, waiting for transfers between devices, shards(): normed_all = lax.all_gather(normed, 'tp', axis=0, tiled=True)  41.2 us
    all_gather x1, waiting for transfers between devices, shards(): cot_all = lax.all_gather(cotangent, 'tp', axis=0, tiled=True)  37.8 us
    reduce_scatter x1, waiting for transfers between devices, shards(): lax.psum_scatter(weight_bc.astype(jnp.bfloat16), 'fsdp', scatter_dimensio...  27.8 us
  transfers between devices with their start and end apart: 13, of which 10 were waited for; matrix products, arithmetic and copies ran while one was open for 21% of the time, Pallas kernels for 0%

commit v1 on v0

--- a/solution.py
+++ b/solution.py
@@ -9,6 +9,13 @@
 INNER = 3072
 EPSILON = 1e-05
 PRECISE = lax.Precision.HIGHEST
+
+
+def _keep_up_row(v0, array_dim):
+    tall = list(v0.shape[1:])
+    tall[array_dim] *= v0.shape[0]
+    z = jnp.moveaxis(v0, 0, array_dim).reshape(tall)
+    return z
 
 
 def causal_conv(signal, kernel, offset_bias, openings):
@@ -128,7 +135,25 @@
     resid = tokens.astype(jnp.float32)
     rstd = lax.rsqrt(jnp.mean(resid * resid, axis=1, keepdims=True) + EPSILON)
     normed = (resid * rstd * norm_gain[None, :]).astype(jnp.bfloat16)
-    normed_all = lax.all_gather(normed, "tp", axis=0, tiled=True)
+    n_blocks = jax.lax.axis_size("tp")
+    pages = [(c, (c + 1) % n_blocks) for c in range(n_blocks)]
+    made = [(q, dev) for dev, q in pages]
+    step_out, o_now = ([], [])
+    for i0 in tuple(range(n_blocks - 1)):
+        if i0 % 2 == 0:
+            step_out.append(
+                jax.lax.ppermute(step_out[-1] if step_out else normed, axis_name="tp", perm=pages)
+            )
+        else:
+            o_now.append(
+                jax.lax.ppermute(o_now[-1] if o_now else normed, axis_name="tp", perm=made)
+            )
+    finding = jnp.stack([*step_out[::-1], normed, *o_now], axis=0)
+    frame_out = jax.lax.axis_index("tp")
+    t1 = len(step_out)
+    front = frame_out - t1
+    finding = finding[(jnp.arange(n_blocks) - front) % n_blocks]
+    normed_all = _keep_up_row(finding, 0)
     pre_z = jnp.dot(normed_all, whole_z, preferred_element_type=jnp.float32)
     pre_x = jnp.dot(normed_all, whole_x, preferred_element_type=jnp.float32)
     pre_bc = jnp.dot(normed_all, whole_bc, preferred_element_type=jnp.float32)

time: 761 us -> 720 us (0.946)
  waiting for transfers between devices: 357 us -> 280 us
  other arithmetic: 78.7 us -> 99.3 us
  local copies, waits for them, and re-layouts: 61.8 us -> 76.6 us
    all_gather x1 -> x0, waiting for transfers between devices: 41.2 us -> none  [shards(): normed_all = lax.all_gather(normed, 'tp', axis=0, tiled=True)]
    all_gather x1, waiting for transfers between devices: 37.8 us -> 0.01 us  [shards(): cot_all = lax.all_gather(cotangent, 'tp', axis=0, tiled=True)]
    ppermute x0 -> x3, waiting for transfers between devices: none -> 24.3 us  [the longest x2 24.3 us: shards(): jax.lax.ppermute(step_out[-1] if step_out else normed, axis_name='tp', pe...]
    all_gather x1, waiting for transfers between devices: 20.3 us -> 0.01 us  [shards(): lax.all_gather(proj_x, 'fsdp', axis=0, tiled=True)]
    dynamic_update_slice x12, other arithmetic: 8.3 us -> 17.3 us  [state_scan(): lax.scan(advance, initial, (openings, carry_decay, block_states))]
  transfers between devices with their start and end apart: 13 -> 15, of which waited for: 10 -> 9; matrix products, arithmetic and copies ran while one was open for 21% -> 28% of each run, Pallas kernels for 0% -> 0%
where the time goes in v1:
time: 720 us; the launch traced here: 715 us
  waiting for transfers between devices  280 us (39%)
  matrix products  155 us (22%)
  other arithmetic  99.3 us (14%)
  blocking collectives  80 us (11%)
  local copies, waits for them, and re-layouts  76.6 us (11%)
  between operations  15.7 us (2%)
  starting transfers between devices  7.55 us (1%)
    reduce_scatter x1, waiting for transfers between devices, shards(): lax.psum_scatter((partial_term(grad_z, whole_z) + partial_term(grad_x, wh...  60.9 us
    dot_general x3, matrix products, state_scan(): jnp.einsum('ctsh,cshp->cthp', weights * intersection[..., None], scaled_x...  47.9 us
    reduce_scatter x1, waiting for transfers between devices, shards(): lax.psum_scatter(weight_z.astype(jnp.bfloat16), 'fsdp', scatter_dimension...  43.9 us
    reduce_scatter x1, waiting for transfers between devices, shards(): lax.psum_scatter(grad_out_rows.astype(jnp.bfloat16), 'fsdp', scatter_dime...  43.9 us
    reduce_scatter x1, waiting for transfers between devices, shards(): lax.psum_scatter(weight_x.astype(jnp.bfloat16), 'fsdp', scatter_dimension...  43.8 us
    reduce_scatter x1, waiting for transfers between devices, shards(): lax.psum_scatter(weight_bc.astype(jnp.bfloat16), 'fsdp', scatter_dimensio...  26.8 us
    psum x1, blocking collectives, shards(): lax.psum((grads[4], grads[5], grads[6], grads[7], grads[8], grads[9], gra...  25.5 us
    ppermute x2, waiting for transfers between devices, shards(): jax.lax.ppermute(step_out[-1] if step_out else normed, axis_name='tp', pe...  24.3 us
  transfers between devices with their start and end apart: 15, of which 9 were waited for; matrix products, arithmetic and copies ran while one was open for 28% of the time, Pallas kernels for 0%

profile of v1, /device:TPU:0, one launch (start us, length us, event | category | flops | bytes accessed | tf_op | source)
XLA Modules:
  0.0 715.1 jit_solution(13209702375002616573)
XLA Ops:
  20.9 9.3 %all-gather = bf16[8,192,12]{1,2,0:T(8,128)(2,1)S(1)} all-gather(bf16[1,192,12]{1,2,0:T(8,128)(2,1)S(1)} %bitcast.226), channel_id=1, replica_groups=mesh['fsdp'=8,'tp'=4] {'fsdp'}, dimensions={0}, use_global_device_ids=true | all-gather | bytes 41472 | tf_op jit(solution)/shard_map/all_gather | solution.py:132
  31.6 13.0 %all_gather.20 = bf16[1536,256]{1,0:T(8,128)(2,1)} all-gather(bf16[192,256]{1,0:T(8,128)(2,1)S(1)} %copy-done.41), channel_id=1, replica_groups=mesh['fsdp'=8,'tp'=4] {'fsdp'}, dimensions={0}, use_global_device_ids=true | all-gather | bytes 884736 | tf_op jit(solution)/shard_map/all_gather | solution.py:131
  57.5 16.4 %collective-permute-done.1 = bf16[256,1536]{1,0:T(8,128)(2,1)S(1)} collective-permute-done((bf16[256,1536]{1,0:T(8,128)(2,1)S(1)}, bf16[256,1536]{1,0:T(8,128)(2,1)S(1)}, u32[]{:S(2)}, u32[]{:S(2)}) %collective-permute-start.1) | collective-permute-done | bytes 786464 | tf_op jit(solution)/shard_map/ppermute | solution.py:145
  119.3 32.4 %while.36 = (s32[]{:T(128)}, f32[12,64,128]{2,1,0:T(8,128)}, f32[4,12,64,128]{3,2,1,0:T(8,128)}, f32[4]{0:T(128)}, f32[4,12,1,1]{1,3,2,0:T(1,128)}, /*index=5*/f...) while((s32[]{:T(128)}, f32[12,64,128]{2,1,0:T(8,128)}, ...), condition=%wide.region_2.3_spmd.clone, body=%wide.region_1.2_spmd.clone.sunk | while | flops 589828 | bytes 1968436 | solution.py:69
  156.2 14.3 %bitcast_add_fusion.3 = f32[4,256,12,64]{1,3,2,0:T(8,128)S(1)} fusion(f32[4,256,12,64]{1,3,2,0:T(8,128)S(1)} %fusion.125, f32[4,256,256]{2,1,0:T(8,128)S(1)} %copy-done.25, f32[4,256,12]{1,2,0:T(8,128)S(1)} %copy-done.29, pred[256,256]{1,0:T(8,128)(4,1)S(1)} %copy-done.44, f32[4,256,12,64]{1,0,3,2:T(4,128)S(1)} %copy-done.3, ...), kind=kOutput, calls=%fused_computation.61 | convolution fusion | flops 2427715584 | bytes 10698752 | tf_op jit(solution)/shard_map/jvp(ctsh,cshp->cthp)/dot_general | solution.py:54
  178.5 8.8 %multiply_reduce_fusion.10 = (f32[1024]{0:T(1024)}, f32[1024,768]{1,0:T(8,128)}, f32[1024,768]{1,0:T(8,128)}) fusion(f32[1024]{0:T(1024)S(1)} %convert_element_type.114, f32[1024,768]{1,0:T(8,128)} %copy.94, f32[1024,768]{1,0:T(8,128)} %get-tuple-element.356, f32[768]{0:T(1024)} %mul.780, bf16[1024,1536]{1,0:T(8,128)(2,1)S(1)} %bitcast.188, ...), kind=kOutput, calls=%fused_computation.78 | convolution fusion | flops 2426928128 | bytes 18099200 | tf_op jit(solution)/shard_map/dot_general | solution.py:157
  187.3 9.1 %psum.105 = f32[1024]{0:T(1024)} all-reduce(f32[1024]{0:T(1024)} %get-tuple-element.353), channel_id=1, replica_groups=mesh['fsdp'=8,'tp'=4] {'tp'}, use_global_device_ids=true, to_apply=%region_4.5 | all-reduce | flops 1024 | bytes 8192 | tf_op jit(solution)/shard_map/psum | solution.py:205
  197.6 8.6 %multiply_reduce_fusion = (f32[768]{0:T(1024)}, f32[1024]{0:T(1024)}, f32[1024,768]{1,0:T(8,128)}) fusion(f32[1024,768]{1,0:T(8,128)} %get-tuple-element.354, f32[1024]{0:T(1024)} %get-tuple-element.382, f32[768]{0:T(1024)} %param.38, bf16[1024,1536]{1,0:T(8,128)(2,1)} %all-gather.12.cloned.1.call-done, bf16[768,1536]{0,1:T(8,128)(2,1)} %all-gather.10.cloned.1.call-done), kind=kOutput, calls=%fused_computation.62 | convolution fusion | flops 2420635904 | bytes 11810816 | tf_op jit(solution)/shard_map/td,cd->tc/dot_general | solution.py:215
  206.2 11.2 %psum.106 = f32[1024]{0:T(1024)} all-reduce(f32[1024]{0:T(1024)} %get-tuple-element.284), channel_id=1, replica_groups=mesh['fsdp'=8,'tp'=4] {'tp'}, use_global_device_ids=true, to_apply=%region_7.8 | all-reduce | flops 1024 | bytes 8192 | tf_op jit(solution)/shard_map/psum | solution.py:220
  218.1 9.1 %multiply_reduce_fusion.1 = (f32[768]{0:T(1024)}, f32[1024,768]{1,0:T(8,128)}, bf16[1024,768]{1,0:T(8,128)(2,1)}) fusion(f32[1024,768]{1,0:T(8,128)} %get-tuple-element.356, f32[1024,768]{1,0:T(8,128)} %get-tuple-element.395, f32[1024]{0:T(1024)S(1)} %convert_element_type.114, f32[1024]{0:T(1024)S(1)} %broadcast_multiply_fusion.1, ...), kind=kLoop, calls=%fused_computation.63 | loop fusion | flops 21232896 | bytes 20472832 | tf_op jit(solution)/shard_map/transpose(jvp())/reduce_sum | solution.py:102
  250.8 25.8 %while.37 = (s32[]{:T(128)}, f32[12,64,128]{2,1,0:T(8,128)S(1)}, f32[4,12]{1,0:T(4,128)}, f32[4,12,64,128]{3,2,1,0:T(8,128)}, f32[4,12,64,128]{3,2,1,0:T(8,128)}...) while((s32[]{:T(128)}, f32[12,64,128]{2,1,0:T(8,128)S(1)}, ...), condition=%wide.region_10.11_spmd.clone, body=%wide.region_8.10_spmd.clone.sunk | while | flops 688120 | bytes 2359756 | solution.py:69
  276.6 8.6 %fusion.70 = f32[4,256,128]{2,1,0:T(8,128)} fusion(f32[4,12,64,128]{3,2,1,0:T(8,128)} %get-tuple-element.224, f32[4,256,12,64]{1,0,3,2:T(4,128)} %reshape.311, f32[4,256,12]{1,2,0:T(8,128)} %get-tuple-element.380, f32[4,256,12]{1,2,0:T(8,128)} %copy.90), kind=kOutput, calls=%fused_computation.129 | convolution fusion | flops 1209532416 | bytes 5341184 | tf_op jit(solution)/shard_map/transpose(jvp(cshp,csn->chpn))/dot_general | solution.py:58
  289.6 18.9 %fusion.14 = (f32[4,256,12]{1,2,0:T(8,128)S(1)}, f32[4,256,12]{1,2,0:T(8,128)}, f32[4,256,256]{2,1,0:T(8,128)}) fusion(f32[4,256,256]{2,1,0:T(8,128)S(1)} %copy-done.26, f32[4,256,12]{1,2,0:T(8,128)S(1)} %copy-done.30, pred[256,256]{1,0:T(8,128)(4,1)S(1)} %copy-done.45, f32[4,256,12,64]{1,0,3,2:T(4,128)S(1)} %copy-done.4, f32[4,256,12]{1,2,0:T(8,128)S(1)} %copy-done.32, ...), kind=kOutput, calls=%fused_computation.26 | convolution fusion | flops 2444730368 | bytes 8650752 | tf_op jit(solution)/shard_map/transpose(jvp(ctsh,cshp->cthp))/dot_general | solution.py:54
  314.8 14.7 %multiply_reduce_fusion.6 = (f32[4,256,12]{1,2,0:T(8,128)S(1)}, f32[4,256,12]{1,2,0:T(8,128)}, f32[4,256,12,64]{1,3,2,0:T(8,128)}) fusion(f32[4,256,12,64]{1,3,2,0:T(8,128)} %fusion.127, f32[4,256,12,64]{1,0,3,2:T(4,128)} %reshape.311, f32[4,256,12]{1,2,0:T(8,128)S(1)} %copy-done.32, f32[4,256,256]{2,1,0:T(8,128)S(1)} %copy-done.27, ...), kind=kOutput, calls=%fused_computation.68 | convolution fusion | flops 2431623168 | bytes 13942784 | tf_op jit(solution)/shard_map/transpose(jvp(ctsh,cshp->cthp))/dot_general | solution.py:54
  341.3 26.8 %reduce-scatter.18.cloned.1.call-done = bf16[192,256]{1,0:T(8,128)(2,1)} async-done(((bf16[1536,256]{1,0:T(8,128)(2,1)}), bf16[192,256]{1,0:T(8,128)(2,1)}) %reduce-scatter.18.cloned.1.call-update) | async-done | bytes 98320 | tf_op jit(solution)/shard_map/reduce_scatter | solution.py:255
  390.9 10.8 %multiply_reduce_fusion.5 = (f32[768]{0:T(1024)S(1)}, f32[768]{0:T(1024)S(1)}, f32[768]{0:T(1024)S(1)}, f32[768]{0:T(1024)S(1)}, f32[768]{0:T(1024)S(1)}, /*index=5*/f32[1024,768]{1,0:T(8,128)S(1)}) fusion(f32[1024,768]{1,0:T(8,128)} %copy-done.12, f32[1024]{0:T(1024)S(1)} %get-tuple-element.384, f32[1024]{0:T(1024)S(1)} %get-tuple-element.383, ...), kind=kLoop, calls=%fused_computation.67 | loop fusion | flops 18870528 | bytes 15763456 | tf_op jit(solution)/shard_map/transpose(jvp())/reduce_sum | solution.py:35
  430.3 12.1 %all-reduce.26.cloned.1.call-done = bf16[192,256]{1,0:T(8,128)(2,1)} async-done(((bf16[192,256]{1,0:T(8,128)(2,1)}), bf16[192,256]{1,0:T(8,128)(2,1)}) %all-reduce.26.cloned.1.call-update) | async-done | bytes 98320 | tf_op jit(solution)/shard_map/psum | solution.py:286
  443.9 43.9 %reduce-scatter.20.cloned.1.call-done = bf16[768,192]{0,1:T(8,128)(2,1)} async-done(((bf16[768,1536]{0,1:T(8,128)(2,1)}), bf16[768,192]{0,1:T(8,128)(2,1)}) %reduce-scatter.20.cloned.1.call-update) | async-done | bytes 294928 | tf_op jit(solution)/shard_map/reduce_scatter | solution.py:261
  489.6 43.9 %reduce-scatter.14.cloned.1.call-done = bf16[192,768]{1,0:T(8,128)(2,1)} async-done(((bf16[1536,768]{1,0:T(8,128)(2,1)}), bf16[192,768]{1,0:T(8,128)(2,1)}) %reduce-scatter.14.cloned.1.call-update) | async-done | bytes 294928 | tf_op jit(solution)/shard_map/reduce_scatter | solution.py:249
  535.4 43.8 %reduce-scatter.16.cloned.1.call-done = bf16[192,768]{1,0:T(8,128)(2,1)} async-done(((bf16[1536,768]{1,0:T(8,128)(2,1)}), bf16[192,768]{1,0:T(8,128)(2,1)}) %reduce-scatter.16.cloned.1.call-update) | async-done | bytes 294928 | tf_op jit(solution)/shard_map/reduce_scatter | solution.py:252
  580.9 60.9 %reduce-scatter.12.cloned.1.call-done = bf16[256,1536]{1,0:T(8,128)(2,1)} async-done(((bf16[1024,1536]{1,0:T(8,128)(2,1)}), bf16[256,1536]{1,0:T(8,128)(2,1)}) %reduce-scatter.12.cloned.1.call-update) | async-done | bytes 786448 | tf_op jit(solution)/shard_map/reduce_scatter | solution.py:237
  643.5 25.5 %all-reduce.22 = (bf16[1536]{0:T(1024)(128)(2,1)S(1)}, f32[4,768]{1,0:T(4,128)}, f32[768]{0:T(1024)}, bf16[4,256]{1,0:T(4,128)(2,1)S(1)}, bf16[256]{0:T(256)(128...) all-reduce(f32[1536]{0:T(1024)S(1)} %get-tuple-element.296, ...), channel_id=1, replica_groups=mesh['fsdp'=8,'tp'=4] {'fsdp'}, use_global_device_ids=true, to_apply=%region_21.22 | all-reduce | flops 7460 | bytes 54048 | tf_op jit(solution)/shard_map/psum | solution.py:271
  668.9 11.9 %all-reduce.23 = (bf16[1536]{0:T(1024)(128)(2,1)S(1)}, bf16[4,256]{1,0:T(4,128)(2,1)S(1)}, bf16[256]{0:T(256)(128)(2,1)S(1)}) all-reduce(bf16[1536]{0:T(1024)(128)(2,1)S(1)} %get-tuple-element.335, bf16[4,256]{1,0:T(4,128)(2,1)S(1)} %get-tuple-element.338, ...), channel_id=1, replica_groups=mesh['fsdp'=8,'tp'=4] {'tp'}, use_global_device_ids=true, to_apply=%region_22.23 | all-reduce | flops 2816 | bytes 11264 | tf_op jit(solution)/shard_map/psum | solution.py:289
  682.6 22.2 %reduce-scatter.10.cloned.1.call-done = bf16[256,1536]{1,0:T(8,128)(2,1)} async-done(((bf16[1024,1536]{1,0:T(8,128)(2,1)}), bf16[256,1536]{1,0:T(8,128)(2,1)}) %reduce-scatter.10.cloned.1.call-update) | async-done | bytes 786448 | tf_op jit(solution)/shard_map/reduce_scatter | solution.py:208
  (355 shorter events, 255.3 us)
Async XLA Ops:
  7.2 49.4 %copy-start.5 = (bf16[256,1536]{1,0:T(8,128)(2,1)S(1)}, bf16[256,1536]{1,0:T(8,128)(2,1)}, u32[]{:S(2)}) copy-start(bf16[256,1536]{1,0:T(8,128)(2,1)} %param.22) | copy-start | bytes 2359300
  7.3 37.3 %copy-start.85 = (f32[12]{0:T(128)S(1)}, f32[12]{0:T(128)}, u32[]{:S(2)}) copy-start(f32[12]{0:T(128)} %param.35) | copy-start | bytes 148
  7.3 37.8 %copy-start.78 = (f32[4,256]{1,0:T(4,128)S(1)}, f32[4,256]{1,0:T(4,128)}, u32[]{:S(2)}) copy-start(f32[4,256]{1,0:T(4,128)} %param.33) | copy-start | bytes 12292
  7.3 86.4 %all-gather.6.cloned.1.call-start = ((), (), s32[]{:S(2)}) async-start(), calls=%async_computation.7 | async-start | bytes 2654208 | tf_op jit(solution)/shard_map/all_gather | solution.py:130
  8.0 170.5 %all-gather.8.cloned.1.call-start = ((), (), s32[]{:S(2)}) async-start(), calls=%async_computation.8 | async-start | bytes 2654208 | tf_op jit(solution)/shard_map/all_gather | solution.py:129
  8.8 188.8 %all-gather.10.cloned.1.call-start = ((), (), s32[]{:S(2)}) async-start(), calls=%async_computation.9 | async-start | bytes 2654208 | tf_op jit(solution)/shard_map/all_gather | solution.py:133
  9.5 188.1 %all-gather.12.cloned.1.call-start = ((), (), s32[]{:S(2)}) async-start(), calls=%async_computation.11 | async-start | bytes 3932160 | tf_op jit(solution)/shard_map/all_gather | solution.py:214
  13.7 43.8 %collective-permute-start.2 = (bf16[256,1536]{1,0:T(8,128)(2,1)}, bf16[256,1536]{1,0:T(8,128)(2,1)S(1)}, u32[]{:S(2)}, u32[]{:S(2)}) collective-permute-start(bf16[256,1536]{1,0:T(8,128)(2,1)} %fusion.54), channel_id=1, source_target_pairs={{1,0},{2,1},{3,2},{0,3},{5,4},{6,5},{7,6},{4,7},{9,8},{10,9},{11,1... | collective-permute-start | bytes 2359304 | tf_op jit(solution)/shard_map/ppermute | solution.py:149
  18.8 34.8 %collective-permute-start = (bf16[256,1536]{1,0:T(8,128)(2,1)}, bf16[256,1536]{1,0:T(8,128)(2,1)S(1)}, u32[]{:S(2)}, u32[]{:S(2)}) collective-permute-start(bf16[256,1536]{1,0:T(8,128)(2,1)} %fusion.54), channel_id=1, source_target_pairs={{0,1},{1,2},{2,3},{3,0},{4,5},{5,6},{6,7},{7,4},{8,9},{9,10},{10,1... | collective-permute-start | bytes 2359304 | tf_op jit(solution)/shard_map/ppermute | solution.py:145
  18.8 349.3 %reduce-scatter.18.cloned.1.call-start = ((), (), s32[]{:S(2)}) async-start(), calls=%async_computation.15 | async-start | bytes 884736 | tf_op jit(solution)/shard_map/reduce_scatter | solution.py:255
  53.6 20.4 %collective-permute-start.1 = (bf16[256,1536]{1,0:T(8,128)(2,1)S(1)}, bf16[256,1536]{1,0:T(8,128)(2,1)S(1)}, u32[]{:S(2)}, u32[]{:S(2)}) collective-permute-start(bf16[256,1536]{1,0:T(8,128)(2,1)S(1)} %collective-permute-done), channel_id=1, source_target_pairs={{0,1},{1,2},{2,3},{3,0},{4,5},{5,6},{6,7},{7,4},{8,9},{9,10},{10,1... | collective-permute-start | bytes 2359304 | tf_op jit(solution)/shard_map/ppermute | solution.py:145
  334.9 93.8 %reduce-scatter.22.cloned.1.call-start = ((), (), s32[]{:S(2)}) async-start(), calls=%async_computation.18 | async-start | bytes 442368
  341.3 101.1 %all-reduce.26.cloned.1.call-start = ((), (), s32[]{:S(2)}) async-start(), calls=%async_computation.16 | async-start | bytes 196608 | tf_op jit(solution)/shard_map/psum | solution.py:286
  368.2 119.7 %reduce-scatter.20.cloned.1.call-start = ((), (), s32[]{:S(2)}) async-start(), calls=%async_computation.17 | async-start | bytes 2654208 | tf_op jit(solution)/shard_map/reduce_scatter | solution.py:261
  375.3 158.3 %reduce-scatter.14.cloned.1.call-start = ((), (), s32[]{:S(2)}) async-start(), calls=%async_computation.13 | async-start | bytes 2654208 | tf_op jit(solution)/shard_map/reduce_scatter | solution.py:249
  380.9 198.2 %reduce-scatter.16.cloned.1.call-start = ((), (), s32[]{:S(2)}) async-start(), calls=%async_computation.14 | async-start | bytes 2654208 | tf_op jit(solution)/shard_map/reduce_scatter | solution.py:252
  409.2 232.7 %reduce-scatter.12.cloned.1.call-start = ((), (), s32[]{:S(2)}) async-start(), calls=%async_computation.12 | async-start | bytes 3932160 | tf_op jit(solution)/shard_map/reduce_scatter | solution.py:237
  420.0 284.8 %reduce-scatter.10.cloned.1.call-start = ((), (), s32[]{:S(2)}) async-start(), calls=%async_computation.10 | async-start | bytes 3932160 | tf_op jit(solution)/shard_map/reduce_scatter | solution.py:208
  427.8 214.1 %copy-start.6 = (bf16[256,1536]{1,0:T(8,128)(2,1)S(1)}, bf16[256,1536]{1,0:T(8,128)(2,1)}, u32[]{:S(2)}) copy-start(bf16[256,1536]{1,0:T(8,128)(2,1)} %param.22) | copy-start | bytes 2359300
  427.8 214.1 %copy-start.40 = (f32[1536]{0:T(1024)S(1)}, f32[1536]{0:T(1024)}, u32[]{:S(2)}) copy-start(f32[1536]{0:T(1024)} %param.26) | copy-start | bytes 18436
  427.8 214.1 %copy-start.58 = (f32[256]{0:T(256)S(1)}, f32[256]{0:T(256)}, u32[]{:S(2)}) copy-start(f32[256]{0:T(256)} %copy-done.57) | copy-start | bytes 3076
  427.8 215.6 %copy-start.76 = (f32[768]{0:T(1024)S(1)}, f32[768]{0:T(1024)}, u32[]{:S(2)}) copy-start(f32[768]{0:T(1024)} %get-tuple-element.283) | copy-start | bytes 9220
  427.8 277.0 %copy-start.18 = (bf16[256,1536]{1,0:T(8,128)(2,1)S(1)}, bf16[256,1536]{1,0:T(8,128)(2,1)}, u32[]{:S(2)}) copy-start(bf16[256,1536]{1,0:T(8,128)(2,1)} %param.23) | copy-start | bytes 2359300
  427.9 277.0 %copy-start.75 = (f32[256]{0:T(256)S(1)}, f32[256]{0:T(256)}, u32[]{:S(2)}) copy-start(f32[256]{0:T(256)} %get-tuple-element.391) | copy-start | bytes 3076
  (78 other events, 525.4 us)
Sparse Core Ops, SparseCore 0:
  10.0 32.9 all-gather.5
  44.8 29.7 all-gather.7
  76.5 28.8 all-gather.9
  106.9 63.4 all-gather.11
  335.1 33.0 reduce-scatter.17
  371.6 33.8 reduce-scatter.21
  407.9 34.4 all-reduce.25
  445.7 42.0 reduce-scatter.19
  491.2 42.3 reduce-scatter.13
  536.7 42.3 reduce-scatter.15
  581.4 60.3 reduce-scatter.11
  644.0 60.7 reduce-scatter.9
